TPU v7x, 32 devices: a whole 2x2x4 slice. The times are simulated.
32 devices in a mesh: expert: 8 (over z, x), shard: 4 (over y, core).
Axes of the slice: x: 2, y: 2, z: 4, core: 2. Of those that a mesh axis runs over, the one named last changes fastest.
Arguments:
- train_down: float32 [16, 6400, 4096], P('expert', None, 'shard'), may hold values from -0.109375 to 0.109375
- router_weight: float32 [4096, 16], P('shard', 'expert'), may hold values from -0.09375 to 0.09375
- router_gain: float32 [4096], P('shard'), may hold values from 0.25 to 1.75
Outputs:
- ready_down: bfloat16 [16, 6400, 4096], P('expert', 'shard')
- scale_down: float32 [16, 6400], P('expert', 'shard')
- serve_router: bfloat16 [4096, 16], replicated
All inputs are finite; a program needn't handle non-finite values. Where the computation divides by a largest or mean magnitude, that divisor is 1e-20 or more.
Results may differ from a plain program's by a relative error of at most 0.001.
Values may be sent and summed in bfloat16 or wider, within the bound.
A program may use at most 192 MiB of HBM per device.

v0:
```python
import jax
import jax.numpy as jnp
from jax import lax
from jax.sharding import PartitionSpec as P


def per_device(train_down, router_weight, router_gain):
    scale_down = lax.pmax(jnp.max(jnp.abs(train_down), axis=2), "shard")
    narrow_down = (train_down / jnp.expand_dims(scale_down, 2)).astype(jnp.bfloat16)
    ready_down = lax.all_to_all(narrow_down, "shard", split_axis=1, concat_axis=2, tiled=True)
    scale_down = lax.dynamic_slice_in_dim(
        scale_down, lax.axis_index("shard") * ready_down.shape[1], ready_down.shape[1], axis=1
    )
    part_router = (router_weight * router_gain[:, None]).astype(jnp.bfloat16)
    row_router = lax.all_gather(part_router, "shard", axis=0, tiled=True)
    serve_router = lax.all_gather(row_router, "expert", axis=1, tiled=True)
    return (ready_down, scale_down, serve_router)


def solution(mesh):
    in_specs = (P("expert", None, "shard"), P("shard", "expert"), P("shard"))
    out_specs = (P("expert", "shard", None), P("expert", "shard"), P())
    return jax.shard_map(
        per_device, mesh=mesh, in_specs=in_specs, out_specs=out_specs, check_vma=False
    )
```

profile of v0, /device:TPU:0, one launch (start us, length us, event | category | flops | bytes accessed | tf_op | source)
XLA Modules:
  0.0 506.3 jit_solution(6970151837764628725)
XLA Ops:
  0.6 17.0 %abs_reduce_fusion = f32[2,6400]{1,0:T(2,128)S(1)} fusion(f32[2,6400,1024]{2,1,0:T(8,128)} %param.3), kind=kLoop, calls=%fused_computation.1 | loop fusion | flops 26201600 | bytes 52480000 | tf_op jit(solution)/shard_map/reduce_max | solution.py:8
  17.6 13.4 %pmax.7 = f32[2,6400]{1,0:T(2,128)S(1)} all-reduce(f32[2,6400]{1,0:T(2,128)S(1)} %abs_reduce_fusion), channel_id=1, replica_groups=mesh['expert'=8,'shard'=4] {'shard'}, use_global_device_ids=true, to_apply=%region_1.0 | all-reduce | flops 12800 | bytes 102400 | tf_op jit(solution)/shard_map/pmax | solution.py:8
  31.1 26.1 %divide_convert_fusion = bf16[2,6400,1024]{2,1,0:T(8,128)(2,1)} fusion(f32[2,6400,1024]{2,1,0:T(8,128)} %param.3, f32[2,6400]{1,0:T(2,128)S(1)} %pmax.7), kind=kLoop, calls=%fused_computation | loop fusion | flops 26214400 | bytes 78694400 | tf_op jit(solution)/shard_map/convert_element_type | solution.py:9
  57.2 0.0 copy-start
  57.2 0.0 copy-start.1
  57.2 47.4 %copy.10 = bf16[2,6400,1024]{2,0,1:T(2,128)(2,1)} copy(bf16[2,6400,1024]{2,1,0:T(8,128)(2,1)} %divide_convert_fusion) | data formatting | bytes 52428800 | tf_op jit(solution)/shard_map/convert_element_type | solution.py:9
  104.6 8.6 %all-to-all-start = ((bf16[2,6400,1024]{2,0,1:T(2,128)(2,1)}), bf16[2,6400,1024]{2,0,1:T(2,128)(2,1)}, u32[]{:S(2)}, u32[]{:S(2)}) async-start(bf16[2,6400,1024]{2,0,1:T(2,128)(2,1)} %copy.10), calls=%async_computation | async-start | bytes 52428800 | tf_op jit(solution)/shard_map/all_to_all | solution.py:10
  113.2 0.0 copy-done
  113.2 0.0 copy-done.1
  113.2 285.0 %all_gather.6 = bf16[4096,2]{0,1:T(2,128)(2,1)S(1)} all-gather(bf16[1024,2]{0,1:T(2,128)(2,1)S(1)} %multiply_convert_fusion), channel_id=1, replica_groups=mesh['expert'=8,'shard'=4] {'shard'}, dimensions={0}, use_global_device_ids=true | all-gather | bytes 20480 | tf_op jit(solution)/shard_map/all_gather | solution.py:15
  398.2 30.8 %all-gather = bf16[8,2,4096]{2,1,0:T(2,128)(2,1)S(1)} all-gather(bf16[1,2,4096]{2,1,0:T(2,128)(2,1)S(1)} %bitcast.8), channel_id=1, replica_groups=mesh['expert'=8,'shard'=4] {'expert'}, dimensions={0}, use_global_device_ids=true | all-gather | bytes 147456 | tf_op jit(solution)/shard_map/all_gather | solution.py:16
  429.1 0.7 reshape.9
  429.8 0.7 constant_dynamic-slice_fusion
  430.5 0.0 all-to-all-done
  430.5 33.4 %copy.11 = bf16[2,1600,4,1024]{3,2,1,0:T(4,128)(2,1)} copy(bf16[2,1600,4,1024]{3,0,1,2:T(2,128)(2,1)} %bitcast.1) | data formatting | bytes 52428800 | tf_op jit(solution)/shard_map/all_to_all | solution.py:10
  463.8 42.5 %all_to_all.16 = bf16[2,1600,4096]{2,1,0:T(8,128)(2,1)} reshape(bf16[2,1600,4,1024]{3,2,1,0:T(4,128)(2,1)} %copy.11) | data formatting | bytes 52428800 | tf_op jit(solution)/shard_map/all_to_all | solution.py:10
  (1 shorter events, 0.0 us)
Async XLA Ops:
  57.2 56.0 %copy-start = (f32[1024,2]{0,1:T(2,128)S(1)}, f32[1024,2]{0,1:T(2,128)}, u32[]{:S(2)}) copy-start(f32[1024,2]{0,1:T(2,128)} %param.4) | copy-start | bytes 24580
  57.2 56.0 %copy-start.1 = (f32[1024]{0:T(1024)S(1)}, f32[1024]{0:T(1024)}, u32[]{:S(2)}) copy-start(f32[1024]{0:T(1024)} %param.5) | copy-start | bytes 12292
  104.6 325.9 %all-to-all-start = ((bf16[2,6400,1024]{2,0,1:T(2,128)(2,1)}), bf16[2,6400,1024]{2,0,1:T(2,128)(2,1)}, u32[]{:S(2)}, u32[]{:S(2)}) async-start(bf16[2,6400,1024]{2,0,1:T(2,128)(2,1)} %copy.10), calls=%async_computation | async-start | bytes 52428800 | tf_op jit(solution)/shard_map/all_to_all | solution.py:10
where the time goes:
time: 508 us; the launch traced here: 506 us
  blocking collectives  329 us (65%)
  local copies, waits for them, and re-layouts  125 us (25%)
  other arithmetic  43.2 us (9%)
  starting transfers between devices  8.59 us (2%)
    all_gather x1, blocking collectives, per_device(): row_router = lax.all_gather(part_router, 'shard', axis=0, tiled=True)  285 us
    all_to_all x2, local copies, waits for them, and re-layouts, per_device(): lax.all_to_all(narrow_down, 'shard', split_axis=1, concat_axis=2, tiled=T...  75.8 us
    convert_element_type x1, local copies, waits for them, and re-layouts, per_device(): (train_down / jnp.expand_dims(scale_down, 2)).astype(jnp.bfloat16)  47.4 us
    all_gather x1, blocking collectives, per_device(): serve_router = lax.all_gather(row_router, 'expert', axis=1, tiled=True)  30.8 us
    convert_element_type x1, other arithmetic, per_device(): (train_down / jnp.expand_dims(scale_down, 2)).astype(jnp.bfloat16)  26.1 us
    reduce_max x1, other arithmetic, per_device(): scale_down = lax.pmax(jnp.max(jnp.abs(train_down), axis=2), 'shard')  17 us
    pmax x1, blocking collectives, per_device(): scale_down = lax.pmax(jnp.max(jnp.abs(train_down), axis=2), 'shard')  13.4 us
  transfers between devices with their start and end apart: 1, of which 0 were waited for; matrix products, arithmetic and copies ran while one was open for 0% of the time, Pallas kernels for 0%

commit v1 on v0

--- a/solution.py
+++ b/solution.py
@@ -1,13 +1,38 @@
+import functools
 import jax
 import jax.numpy as jnp
 from jax import lax
 from jax.sharding import PartitionSpec as P
 
 
+def find_the_field(piece_in, across):
+    seen_now = lax.axis_size(across)
+    earlier = lax.axis_index(across)
+    side_arr, part_now = (seen_now, earlier)
+    lower = piece_in.shape[1] // side_arr
+    outer = list(piece_in.shape)
+    outer[1] = lower
+    low = outer[2]
+    outer[2] = low * side_arr
+    arr_now = jnp.zeros(outer, piece_in.dtype)
+    b = 0
+    while b < side_arr:
+        a_next = lax.dynamic_slice_in_dim(piece_in, (part_now ^ b) * lower, lower, axis=1)
+        if b:
+            extra = tuple(((j, j ^ b) for j in range(side_arr)))
+            a_next = lax.ppermute(a_next, across, extra)
+        arr_now = lax.dynamic_update_slice_in_dim(arr_now, a_next, (part_now ^ b) * low, axis=2)
+        b += 1
+    return arr_now
+
+
+cover_outputs = functools.partial(find_the_field, across="shard")
+
+
 def per_device(train_down, router_weight, router_gain):
     scale_down = lax.pmax(jnp.max(jnp.abs(train_down), axis=2), "shard")
     narrow_down = (train_down / jnp.expand_dims(scale_down, 2)).astype(jnp.bfloat16)
-    ready_down = lax.all_to_all(narrow_down, "shard", split_axis=1, concat_axis=2, tiled=True)
+    ready_down = cover_outputs(narrow_down)
     scale_down = lax.dynamic_slice_in_dim(
         scale_down, lax.axis_index("shard") * ready_down.shape[1], ready_down.shape[1], axis=1
     )

time: 508 us -> 422 us (0.83)
  local copies, waits for them, and re-layouts: 125 us -> 48.7 us
  starting transfers between devices: 8.59 us -> 1.86 us
    all_to_all x2 -> x0, local copies, waits for them, and re-layouts: 75.8 us -> none  [per_device(): lax.all_to_all(narrow_down, 'shard', split_axis=1, concat_axis=2, tiled=T...]
    convert_element_type x1 -> x0, local copies, waits for them, and re-layouts: 47.4 us -> none  [per_device(): (train_down / jnp.expand_dims(scale_down, 2)).astype(jnp.bfloat16)]
    dynamic_update_slice x0 -> x3, local copies, waits for them, and re-layouts: none -> 19.2 us  [find_the_field(): lax.dynamic_update_slice_in_dim(arr_now, a_next, (part_now ^ b) * low, ax...]
    dynamic_slice x0 -> x1, local copies, waits for them, and re-layouts: none -> 19.2 us  [find_the_field(): lax.dynamic_slice_in_dim(piece_in, (part_now ^ b) * lower, lower, axis=1)]
    broadcast_in_dim x0 -> x1, local copies, waits for them, and re-layouts: none -> 8.97 us  [find_the_field(): arr_now = jnp.zeros(outer, piece_in.dtype)]
    all_to_all x1 -> x0, starting transfers between devices: 8.59 us -> none  [per_device(): lax.all_to_all(narrow_down, 'shard', split_axis=1, concat_axis=2, tiled=T...]
  transfers between devices with their start and end apart: 1 -> 3, of which waited for: 0 -> 0; matrix products, arithmetic and copies ran while one was open for 0% -> 3% of each run, Pallas kernels for 0% -> 0%
where the time goes in v1:
time: 422 us
  blocking collectives  328 us (78%)
  local copies, waits for them, and re-layouts  48.7 us (12%)
  other arithmetic  43.2 us (10%)
    all_gather x1, blocking collectives, per_device(): row_router = lax.all_gather(part_router, 'shard', axis=0, tiled=True)  283 us
    all_gather x1, blocking collectives, per_device(): serve_router = lax.all_gather(row_router, 'expert', axis=1, tiled=True)  30.8 us
    convert_element_type x1, other arithmetic, per_device(): (train_down / jnp.expand_dims(scale_down, 2)).astype(jnp.bfloat16)  26.2 us
    dynamic_update_slice x3, local copies, waits for them, and re-layouts, find_the_field(): lax.dynamic_update_slice_in_dim(arr_now, a_next, (part_now ^ b) * low, ax...  19.2 us
    dynamic_slice x1, local copies, waits for them, and re-layouts, find_the_field(): lax.dynamic_slice_in_dim(piece_in, (part_now ^ b) * lower, lower, axis=1)  19.2 us
    reduce_max x1, other arithmetic, per_device(): scale_down = lax.pmax(jnp.max(jnp.abs(train_down), axis=2), 'shard')  17 us
    pmax x1, blocking collectives, per_device(): scale_down = lax.pmax(jnp.max(jnp.abs(train_down), axis=2), 'shard')  13.4 us
    broadcast_in_dim x1, local copies, waits for them, and re-layouts, find_the_field(): arr_now = jnp.zeros(outer, piece_in.dtype)  8.97 us
  transfers between devices with their start and end apart: 3, of which 0 were waited for; matrix products, arithmetic and copies ran while one was open for 3% of the time, Pallas kernels for 0%

profile of v1, /device:TPU:0, one launch (start us, length us, event | category | flops | bytes accessed | tf_op | source)
XLA Modules:
  0.0 422.1 jit_solution(469577618475261511)
XLA Ops:
  0.6 17.0 %abs_reduce_fusion = f32[2,6400]{1,0:T(2,128)S(1)} fusion(f32[2,6400,1024]{2,1,0:T(8,128)} %param.3), kind=kLoop, calls=%fused_computation.1 | loop fusion | flops 26201600 | bytes 52480000 | tf_op jit(solution)/shard_map/reduce_max | solution.py:33
  17.7 13.4 %pmax.7 = f32[2,6400]{1,0:T(2,128)S(1)} all-reduce(f32[2,6400]{1,0:T(2,128)S(1)} %abs_reduce_fusion), channel_id=1, replica_groups=mesh['expert'=8,'shard'=4] {'shard'}, use_global_device_ids=true, to_apply=%region_1.0 | all-reduce | flops 12800 | bytes 102400 | tf_op jit(solution)/shard_map/pmax | solution.py:33
  31.1 26.2 %divide_convert_fusion = bf16[2,6400,1024]{2,1,0:T(8,128)(2,1)} fusion(f32[2,6400,1024]{2,1,0:T(8,128)} %param.3, f32[2,6400]{1,0:T(2,128)S(1)} %pmax.7), kind=kLoop, calls=%fused_computation | loop fusion | flops 26214400 | bytes 78694400 | tf_op jit(solution)/shard_map/convert_element_type | solution.py:34
  57.3 9.0 %broadcast_in_dim.2 = bf16[2,1600,4096]{2,1,0:T(8,128)(2,1)} broadcast(bf16[]{:T(256)} %constant.11.clone.1), dimensions={} | broadcast | bytes 26214402 | tf_op jit(solution)/shard_map/broadcast_in_dim | solution.py:17
  66.3 0.0 copy-start
  66.3 0.0 copy-start.1
  66.3 19.2 %constant_dynamic-slice_fusion = (bf16[2,1600,1024]{2,1,0:T(8,128)(2,1)}, bf16[2,1600,1024]{2,1,0:T(8,128)(2,1)}, bf16[2,1600,1024]{2,1,0:T(8,128)(2,1)}, bf16[2,1600,4096]{2,1,0:T(8,128)(2,1)}) fusion(bf16[2,6400,1024]{2,1,0:T(8,128)(2,1)} %divide_convert_fusion, s32[]{:T(128)S(6)} %select_n.31, s32[]{:T(128)S(6)} %select_n.29, s32[]{:T(128)S(6)} %select_n.27, ...), kind=kLoop, calls=%fused_computation.5 | loop fusion | bytes 52428820 | tf_op jit(solution)/shard_map/dynamic_slice | solution.py:20
  85.4 0.0 collective-permute-start
  85.4 0.4 collective-permute-start.1
  85.9 1.4 collective-permute-start.2
  87.3 0.0 copy-done
  87.3 0.0 copy-done.1
  87.3 283.3 %all_gather.6 = bf16[4096,2]{0,1:T(2,128)(2,1)S(1)} all-gather(bf16[1024,2]{0,1:T(2,128)(2,1)S(1)} %multiply_convert_fusion), channel_id=1, replica_groups=mesh['expert'=8,'shard'=4] {'shard'}, dimensions={0}, use_global_device_ids=true | all-gather | bytes 20480 | tf_op jit(solution)/shard_map/all_gather | solution.py:40
  370.6 30.8 %all-gather = bf16[8,2,4096]{2,1,0:T(2,128)(2,1)S(1)} all-gather(bf16[1,2,4096]{2,1,0:T(2,128)(2,1)S(1)} %bitcast.5), channel_id=1, replica_groups=mesh['expert'=8,'shard'=4] {'expert'}, dimensions={0}, use_global_device_ids=true | all-gather | bytes 147456 | tf_op jit(solution)/shard_map/all_gather | solution.py:41
  401.5 0.7 reshape.9
  402.2 0.7 constant_dynamic-slice_fusion.3
  402.9 0.0 collective-permute-done
  402.9 6.4 %constant_dynamic-update-slice_fusion.2 = bf16[2,1600,4096]{2,1,0:T(8,128)(2,1)} fusion(bf16[2,1600,4096]{2,1,0:T(8,128)(2,1)} %get-tuple-element.6, bf16[2,1600,1024]{2,1,0:T(8,128)(2,1)} %collective-permute-done, s32[]{:T(128)S(6)} %select_n.28), kind=kLoop, calls=%fused_computation.8 | loop fusion | bytes 13107204 | tf_op jit(solution)/shard_map/dynamic_update_slice | solution.py:24
  409.3 0.0 collective-permute-done.1
  409.3 6.4 %constant_dynamic-update-slice_fusion.1 = bf16[2,1600,4096]{2,1,0:T(8,128)(2,1)} fusion(bf16[2,1600,4096]{2,1,0:T(8,128)(2,1)} %constant_dynamic-update-slice_fusion.2, bf16[2,1600,1024]{2,1,0:T(8,128)(2,1)} %collective-permute-done.1, s32[]{:T(128)S(6)} %select_n.30), kind=kLoop, calls=%fused_computation.6 | loop fusion | bytes 13107204 | tf_op jit(solution)/shard_map/dynamic_update_slice | solution.py:24
  415.7 0.0 collective-permute-done.2
  415.7 6.4 %constant_dynamic-update-slice_fusion = bf16[2,1600,4096]{2,1,0:T(8,128)(2,1)} fusion(bf16[2,1600,4096]{2,1,0:T(8,128)(2,1)} %constant_dynamic-update-slice_fusion.1, bf16[2,1600,1024]{2,1,0:T(8,128)(2,1)} %collective-permute-done.2, s32[]{:T(128)S(6)} %select_n.32), kind=kLoop, calls=%fused_computation.4 | loop fusion | bytes 13107204 | tf_op jit(solution)/shard_map/dynamic_update_slice | solution.py:24
  (1 shorter events, 0.0 us)
Async XLA Ops:
  66.3 21.0 %copy-start = (f32[1024,2]{0,1:T(2,128)S(1)}, f32[1024,2]{0,1:T(2,128)}, u32[]{:S(2)}) copy-start(f32[1024,2]{0,1:T(2,128)} %param.4) | copy-start | bytes 24580
  66.3 21.0 %copy-start.1 = (f32[1024]{0:T(1024)S(1)}, f32[1024]{0:T(1024)}, u32[]{:S(2)}) copy-start(f32[1024]{0:T(1024)} %param.5) | copy-start | bytes 12292
  85.4 317.5 %collective-permute-start = (bf16[2,1600,1024]{2,1,0:T(8,128)(2,1)}, bf16[2,1600,1024]{2,1,0:T(8,128)(2,1)}, u32[]{:S(2)}, u32[]{:S(2)}) collective-permute-start(bf16[2,1600,1024]{2,1,0:T(8,128)(2,1)} %get-tuple-element.5), channel_id=1, source_target_pairs={{0,1},{1,0},{2,3},{3,2},{4,5},{5,4},{6,7},{7,6},{8,9},{9,8},{10,11... | collective-permute-start | bytes 19660808 | tf_op jit(solution)/shard_map/ppermute | solution.py:23
  85.4 323.8 %collective-permute-start.1 = (bf16[2,1600,1024]{2,1,0:T(8,128)(2,1)}, bf16[2,1600,1024]{2,1,0:T(8,128)(2,1)}, u32[]{:S(2)}, u32[]{:S(2)}) collective-permute-start(bf16[2,1600,1024]{2,1,0:T(8,128)(2,1)} %get-tuple-element.4), channel_id=1, source_target_pairs={{0,2},{1,3},{2,0},{3,1},{4,6},{5,7},{6,4},{7,5},{8,10},{9,11},{10,... | collective-permute-start | bytes 19660808 | tf_op jit(solution)/shard_map/ppermute | solution.py:23
  85.9 329.8 %collective-permute-start.2 = (bf16[2,1600,1024]{2,1,0:T(8,128)(2,1)}, bf16[2,1600,1024]{2,1,0:T(8,128)(2,1)}, u32[]{:S(2)}, u32[]{:S(2)}) collective-permute-start(bf16[2,1600,1024]{2,1,0:T(8,128)(2,1)} %get-tuple-element.3), channel_id=1, source_target_pairs={{0,3},{1,2},{2,1},{3,0},{4,7},{5,6},{6,5},{7,4},{8,11},{9,10},{10,... | collective-permute-start | bytes 19660808 | tf_op jit(solution)/shard_map/ppermute | solution.py:23
